TPU v7x, 32 devices: a whole 2x2x4 slice. The times are simulated.
32 devices in a mesh: pipe: 2 (over core), dp: 8 (over z, y), mp: 2 (over x).
Axes of the slice: x: 2, y: 2, z: 4, core: 2. Of those that a mesh axis runs over, the one named last changes fastest.
Arguments:
- token_ids: int32 [2, 4096], P('pipe', 'dp'), may hold values from 0 to 32127, as said below
- embedded: bfloat16 [2, 4096, 4096], P('pipe', 'dp', 'mp'), may hold values from -720 to 720
- norm_gain: float32 [2, 4096], P('pipe', 'mp'), may hold values from 0.25 to 1.75
- proj_grad: bfloat16 [2, 4096, 2048], P('pipe', 'dp'), may hold values from -6 to 6
- proj_weight: bfloat16 [2, 4096, 2048], P('pipe', 'mp'), may hold values from -0.125 to 0.125
- stream_grad: bfloat16 [2, 4096, 4096], P('pipe', 'dp', 'mp'), may hold values from -6 to 6
Outputs:
- table_grad: float32 [32128, 2, 2048], P('dp', 'mp', 'pipe')
Inputs may be any that keep to these rules, and one draw needn't show every extreme that they name: `token_ids`: call block o the ids o * 4016 to (o + 1) * 4016 - 1. The 512 tokens of one stack on one index of dp hold at most 128 ids of any one block, and some block gets exactly 128 of them.
All inputs are finite; a program needn't handle non-finite values.
Results may differ from a plain program's by a relative error of at most 0.0029.
Values may be sent and summed in bfloat16 or wider, within the bound.
A program may use at most 128 MiB of HBM per device.

v0:
```python
import jax
import jax.numpy as jnp
from jax import lax
from jax.sharding import PartitionSpec as P

D = 4096
VOCAB = 32128
epsilon = 1e-06


def accumulate(got_rows, got_index, block_rows):
    width = got_rows.shape[-1]
    flat_rows = got_rows.reshape(-1, width)
    flat_index = got_index.reshape(-1)
    selector = (flat_index[None, :] == jnp.arange(block_rows, dtype=jnp.int32)[:, None]).astype(
        jnp.bfloat16
    )
    return jnp.dot(selector, flat_rows, preferred_element_type=jnp.float32)


def on_device(token_ids, embedded, norm_gain, proj_grad, proj_weight, stream_grad):
    projected = lax.dot_general(
        proj_grad[0], proj_weight[0], (((1,), (1,)), ((), ())), preferred_element_type=jnp.float32
    )
    inputs = embedded[0].astype(jnp.float32)
    scaled = projected * norm_gain[0][None, :]
    square_sum, mixed_sum = lax.psum(
        (jnp.sum(inputs * inputs, axis=1), jnp.sum(inputs * scaled, axis=1)), "mp"
    )
    inverse = lax.rsqrt(square_sum / D + epsilon)
    norm_back = (
        inverse[:, None] * scaled - inputs * (inverse * inverse * inverse * mixed_sum / D)[:, None]
    )
    grad_rows = (stream_grad[0].astype(jnp.float32) + norm_back).astype(jnp.bfloat16)
    replicas = lax.axis_size("dp")
    tokens_here = grad_rows.shape[0]
    capacity = max(2, 2 * tokens_here // replicas)
    block_rows = VOCAB // replicas
    token_row = token_ids[0]
    owners = token_row // block_rows
    local_row = token_row % block_rows
    matches = (owners[:, None] == jnp.arange(replicas, dtype=jnp.int32)[None, :]).astype(jnp.int32)
    earlier = jnp.cumsum(matches, axis=0) - matches
    position = owners * capacity + jnp.sum(earlier * matches, axis=1)
    placer = (
        position[None, :] == jnp.arange(replicas * capacity, dtype=jnp.int32)[:, None]
    ).astype(jnp.bfloat16)
    send_rows = jnp.dot(placer, grad_rows, preferred_element_type=jnp.float32).astype(jnp.bfloat16)
    send_rows = send_rows.reshape(replicas, capacity, grad_rows.shape[1])
    send_index = jnp.full((replicas * capacity,), block_rows, jnp.int32).at[position].set(local_row)
    send_index = send_index.reshape(replicas, capacity)
    paired_index = jnp.stack([send_index, send_index], axis=2)
    mixed_rows, mixed_index = (
        lax.all_to_all(send_rows, "pipe", split_axis=2, concat_axis=1, tiled=True),
        lax.all_to_all(paired_index, "pipe", split_axis=2, concat_axis=1, tiled=True),
    )
    got_rows, got_index = (
        lax.all_to_all(mixed_rows, "dp", split_axis=0, concat_axis=0, tiled=True),
        lax.all_to_all(mixed_index, "dp", split_axis=0, concat_axis=0, tiled=True),
    )
    half_table = accumulate(got_rows, got_index, block_rows)
    return half_table.reshape(block_rows, 1, half_table.shape[1])


def solution(mesh):
    return jax.shard_map(
        on_device,
        mesh=mesh,
        in_specs=(
            P("pipe", "dp"),
            P("pipe", "dp", "mp"),
            P("pipe", "mp"),
            P("pipe", "dp", None),
            P("pipe", "mp", None),
            P("pipe", "dp", "mp"),
        ),
        out_specs=P("dp", "mp", "pipe"),
        check_vma=False,
    )
```

profile of v0, /device:TPU:0, one launch (start us, length us, event | category | flops | bytes accessed | tf_op | source)
XLA Modules:
  0.0 245.0 jit_solution(3031371806581677621)
XLA Ops:
  0.0 0.0 copy-start
  0.0 0.9 compare_reduce_fusion
  0.9 0.7 broadcast_remainder_fusion
  1.6 1.1 reduce-window.6
  2.7 0.2 slice_reduce_fusion
  3.0 0.1 fusion.19
  3.1 0.7 compare_select_fusion
  3.8 2.4 scatter_custom_fusion
  6.3 0.6 pad_add_fusion
  6.8 3.2 %all-to-all-start = ((s32[8,128,2]{1,0,2:T(8,128)}), s32[8,128,2]{1,0,2:T(8,128)S(1)}, u32[]{:S(2)}, u32[]{:S(2)}) async-start(s32[8,128,2]{1,0,2:T(8,128)} %pad_add_fusion), calls=%async_computation | async-start | bytes 16384 | tf_op jit(solution)/shard_map/all_to_all | solution.py:55
  10.1 0.7 fusion.22
  10.8 0.0 copy-done
  10.8 0.0 copy-start.2
  10.8 10.0 %fusion.5 = (f32[512]{0:T(512)S(1)}, f32[512]{0:T(512)S(1)}, f32[512,2048]{1,0:T(8,128)}) fusion(bf16[1,512,2048]{2,1,0:T(8,128)(2,1)} %param.7, f32[2048]{0:T(1024)} %bitcast.84, bf16[1,2048,2048]{2,1,0:T(8,128)(2,1)} %param.10, bf16[1,512,2048]{2,1,0:T(8,128)(2,1)S(1)} %copy-done), kind=kOutput, calls=%fused_computation.10 | convolution fusion | flops 4301257728 | bytes 16789504 | tf_op jit(solution)/shard_map/dot_general | solution.py:22
  20.8 5.8 %all-reduce = (f32[512]{0:T(512)S(1)}, f32[512]{0:T(512)S(1)}) all-reduce(f32[512]{0:T(512)S(1)} %get-tuple-element.6, f32[512]{0:T(512)S(1)} %get-tuple-element.5), channel_id=1, replica_groups=mesh['pipe'=2,'dp'=8,'mp'=2] {'mp'}, use_global_device_ids=true, to_apply=%region_7.8 | all-reduce | flops 1024 | bytes 8192 | tf_op jit(solution)/shard_map/psum | solution.py:27
  26.7 0.0 copy-done.2
  26.7 8.1 %convolution_convert_fusion = bf16[1024,2048]{1,0:T(8,128)(2,1)} fusion(f32[512,2048]{1,0:T(8,128)} %get-tuple-element.17, bf16[1,512,2048]{2,1,0:T(8,128)(2,1)} %param.11, bf16[1,512,2048]{2,1,0:T(8,128)(2,1)} %param.7, f32[512]{0:T(512)S(1)} %get-tuple-element.16, f32[2048]{0:T(1024)S(1)} %bitcast.85, f32[512]{0:T(512)S(1)} %get-tuple-element.15, ...), kind=kOutput, calls=%fused_computation.15 | convolution fusion | flops 2158493696 | bytes 12597248 | tf_op jit(solution)/shard_map/dot_general | solution.py:48
  34.8 6.8 %copy.13 = bf16[8,128,2048]{1,0,2:T(8,128)(2,1)} copy(bf16[8,128,2048]{2,1,0:T(8,128)(2,1)} %bitcast.72) | data formatting | bytes 8388608 | tf_op jit(solution)/shard_map/reshape | solution.py:49
  41.6 0.0 all-to-all-done
  41.6 5.6 %all-to-all-start.2 = ((bf16[8,128,2048]{1,0,2:T(8,128)(2,1)}), bf16[8,128,2048]{1,0,2:T(8,128)(2,1)}, u32[]{:S(2)}, u32[]{:S(2)}) async-start(bf16[8,128,2048]{1,0,2:T(8,128)(2,1)} %copy.13), calls=%async_computation.2 | async-start | bytes 8388608 | tf_op jit(solution)/shard_map/all_to_all | solution.py:54
  47.2 0.6 copy.12
  47.8 3.9 %all-to-all-done.2 = bf16[8,128,2048]{1,0,2:T(8,128)(2,1)} async-done(((bf16[8,128,2048]{1,0,2:T(8,128)(2,1)}), bf16[8,128,2048]{1,0,2:T(8,128)(2,1)}, u32[]{:S(2)}, u32[]{:S(2)}) %all-to-all-start.2) | async-done | bytes 4194336 | tf_op jit(solution)/shard_map/all_to_all | solution.py:54
  51.7 6.4 %all-to-all-start.1 = ((s32[8,256,1]{1,2,0:T(1,128)}), s32[8,256,1]{1,2,0:T(1,128)S(1)}, u32[]{:S(2)}, u32[]{:S(2)}) async-start(s32[8,256,1]{1,2,0:T(1,128)} %copy.12), calls=%async_computation.1 | async-start | bytes 16384 | tf_op jit(solution)/shard_map/all_to_all | solution.py:59
  58.0 6.6 %copy.15 = bf16[8,2,128,1024]{3,2,1,0:T(8,128)(2,1)} copy(bf16[8,2,128,1024]{2,0,3,1:T(8,128)(2,1)} %bitcast.25) | data formatting | bytes 8388608 | tf_op jit(solution)/shard_map/all_to_all | solution.py:54
  64.6 0.0 all-to-all-done.1
  64.6 99.1 %all_to_all.46 = bf16[8,256,1024]{2,1,0:T(8,128)(2,1)S(1)} all-to-all(bf16[8,256,1024]{2,1,0:T(8,128)(2,1)} %bitcast.71), channel_id=1, replica_groups=mesh['pipe'=2,'dp'=8,'mp'=2] {'dp'}, dimensions={0} | all-to-all | bytes 8388608 | tf_op jit(solution)/shard_map/all_to_all | solution.py:58
  163.8 17.4 %fusion.2 = f32[4016,1,1024]{2,0,1:T(8,128)S(1)} fusion(bf16[2048,1024]{1,0:T(8,128)(2,1)S(1)} %bitcast.73, s32[2048]{0:T(1024)S(1)} %bitcast.81), kind=kOutput, calls=%fused_computation.4 | convolution fusion | flops 16852549632 | bytes 20652032 | tf_op jit(solution)/shard_map/dot_general | solution.py:18
  181.1 0.0 copy-start.1
  181.2 63.9 %copy.16 = f32[4016,1,1024]{2,1,0:T(1,128)} copy(f32[4016,1,1024]{2,0,1:T(8,128)S(1)} %fusion.2) | data formatting | bytes 32899072 | tf_op jit(solution)/shard_map/reshape | solution.py:62
  245.0 0.0 copy-done.1
  (6 shorter events, 0.1 us)
Async XLA Ops:
  0.0 10.8 %copy-start = (bf16[1,512,2048]{2,1,0:T(8,128)(2,1)S(1)}, bf16[1,512,2048]{2,1,0:T(8,128)(2,1)}, u32[]{:S(2)}) copy-start(bf16[1,512,2048]{2,1,0:T(8,128)(2,1)} %param.9) | copy-start | bytes 6291460
  6.8 34.7 %all-to-all-start = ((s32[8,128,2]{1,0,2:T(8,128)}), s32[8,128,2]{1,0,2:T(8,128)S(1)}, u32[]{:S(2)}, u32[]{:S(2)}) async-start(s32[8,128,2]{1,0,2:T(8,128)} %pad_add_fusion), calls=%async_computation | async-start | bytes 16384 | tf_op jit(solution)/shard_map/all_to_all | solution.py:55
  10.8 15.9 %copy-start.2 = (f32[1,2048]{1,0:T(1,128)S(1)}, f32[1,2048]{1,0:T(1,128)}, u32[]{:S(2)}) copy-start(f32[1,2048]{1,0:T(1,128)} %param.8) | copy-start | bytes 24580
  41.6 10.1 %all-to-all-start.2 = ((bf16[8,128,2048]{1,0,2:T(8,128)(2,1)}), bf16[8,128,2048]{1,0,2:T(8,128)(2,1)}, u32[]{:S(2)}, u32[]{:S(2)}) async-start(bf16[8,128,2048]{1,0,2:T(8,128)(2,1)} %copy.13), calls=%async_computation.2 | async-start | bytes 8388608 | tf_op jit(solution)/shard_map/all_to_all | solution.py:54
  51.7 13.0 %all-to-all-start.1 = ((s32[8,256,1]{1,2,0:T(1,128)}), s32[8,256,1]{1,2,0:T(1,128)S(1)}, u32[]{:S(2)}, u32[]{:S(2)}) async-start(s32[8,256,1]{1,2,0:T(1,128)} %copy.12), calls=%async_computation.1 | async-start | bytes 16384 | tf_op jit(solution)/shard_map/all_to_all | solution.py:59
  181.1 63.9 %copy-start.1 = (bf16[1,512,2048]{2,1,0:T(8,128)(2,1)S(1)}, bf16[1,512,2048]{2,1,0:T(8,128)(2,1)}, u32[]{:S(2)}) copy-start(bf16[1,512,2048]{2,1,0:T(8,128)(2,1)} %param.9) | copy-start | bytes 6291460
where the time goes:
time: 246 us; the launch traced here: 245 us
  blocking collectives  105 us (43%)
  local copies, waits for them, and re-layouts  80.5 us (33%)
  matrix products  35.5 us (14%)
  starting transfers between devices  15.2 us (6%)
  other arithmetic  4.86 us (2%)
  waiting for transfers between devices  3.88 us (2%)
    all_to_all x1, blocking collectives, on_device(): lax.all_to_all(mixed_rows, 'dp', split_axis=0, concat_axis=0, tiled=True)  99.1 us
    reshape x1, local copies, waits for them, and re-layouts, on_device(): return half_table.reshape(block_rows, 1, half_table.shape[1])  63.9 us
    dot_general x1, matrix products, accumulate(): return jnp.dot(selector, flat_rows, preferred_element_type=jnp.float32)  17.4 us
    dot_general x1, matrix products, on_device(): lax.dot_general(proj_grad[0], proj_weight[0], (((1,), (1,)), ((), ())), p...  10 us
    dot_general x1, matrix products, on_device(): jnp.dot(placer, grad_rows, preferred_element_type=jnp.float32)  8.1 us
    reshape x1, local copies, waits for them, and re-layouts, on_device(): send_rows = send_rows.reshape(replicas, capacity, grad_rows.shape[1])  6.76 us
    all_to_all x1, local copies, waits for them, and re-layouts, on_device(): lax.all_to_all(send_rows, 'pipe', split_axis=2, concat_axis=1, tiled=True)  6.6 us
    all_to_all x1, starting transfers between devices, on_device(): lax.all_to_all(mixed_index, 'dp', split_axis=0, concat_axis=0, tiled=True)  6.37 us
  transfers between devices with their start and end apart: 3, of which 1 were waited for; matrix products, arithmetic and copies ran while one was open for 13% of the time, Pallas kernels for 0%

commit v1 on v0

--- a/solution.py
+++ b/solution.py
@@ -51,7 +51,12 @@
     send_index = send_index.reshape(replicas, capacity)
     paired_index = jnp.stack([send_index, send_index], axis=2)
     mixed_rows, mixed_index = (
-        lax.all_to_all(send_rows, "pipe", split_axis=2, concat_axis=1, tiled=True),
+        jnp.concatenate(
+            lax.all_to_all(
+                jnp.stack(jnp.split(send_rows, lax.axis_size("pipe"), axis=2)), "pipe", 0, 0
+            ),
+            axis=1,
+        ),
         lax.all_to_all(paired_index, "pipe", split_axis=2, concat_axis=1, tiled=True),
     )
     got_rows, got_index = (

time: 246 us -> 238 us (0.967)
  local copies, waits for them, and re-layouts: 80.5 us -> 72.4 us
    reshape x1 -> x0, local copies, waits for them, and re-layouts: 6.76 us -> none  [on_device(): send_rows = send_rows.reshape(replicas, capacity, grad_rows.shape[1])]
  transfers between devices with their start and end apart: 3 -> 3, of which waited for: 1 -> 2; matrix products, arithmetic and copies ran while one was open for 13% -> 11% of each run, Pallas kernels for 0% -> 0%
where the time goes in v1:
time: 238 us; the launch traced here: 237 us
  blocking collectives  103 us (43%)
  local copies, waits for them, and re-layouts  72.4 us (30%)
  matrix products  33.6 us (14%)
  starting transfers between devices  15.2 us (6%)
  other arithmetic  7.23 us (3%)
  waiting for transfers between devices  5.59 us (2%)
    all_to_all x1, blocking collectives, on_device(): lax.all_to_all(mixed_rows, 'dp', split_axis=0, concat_axis=0, tiled=True)  97.4 us
    reshape x1, local copies, waits for them, and re-layouts, on_device(): return half_table.reshape(block_rows, 1, half_table.shape[1])  63.9 us
    dot_general x1, matrix products, accumulate(): return jnp.dot(selector, flat_rows, preferred_element_type=jnp.float32)  17.4 us
    dot_general x1, matrix products, on_device(): lax.dot_general(proj_grad[0], proj_weight[0], (((1,), (1,)), ((), ())), p...  10 us
    all_to_all x1, starting transfers between devices, on_device(): lax.all_to_all(mixed_index, 'dp', split_axis=0, concat_axis=0, tiled=True)  6.38 us
    dot_general x1, matrix products, on_device(): jnp.dot(placer, grad_rows, preferred_element_type=jnp.float32)  6.18 us
    psum x1, blocking collectives, on_device(): lax.psum((jnp.sum(inputs * inputs, axis=1), jnp.sum(inputs * scaled, axis...  5.84 us
    all_to_all x1, starting transfers between devices, on_device(): lax.all_to_all(jnp.stack(jnp.split(send_rows, lax.axis_size('pipe'), axis...  5.62 us
  transfers between devices with their start and end apart: 3, of which 2 were waited for; matrix products, arithmetic and copies ran while one was open for 11% of the time, Pallas kernels for 0%

profile of v1, /device:TPU:0, one launch (start us, length us, event | category | flops | bytes accessed | tf_op | source)
XLA Modules:
  0.0 237.4 jit_solution(5326881770113705145)
XLA Ops:
  0.0 0.0 copy-start
  0.0 0.9 compare_reduce_fusion
  0.9 0.7 broadcast_remainder_fusion
  1.6 1.1 reduce-window.6
  2.7 0.2 slice_reduce_fusion
  3.0 0.1 fusion.19
  3.1 0.7 compare_select_fusion
  3.8 2.4 %scatter_custom_fusion = s32[1024]{0:T(1024)S(1)} fusion(s32[512]{0:T(512)S(1)} %bitcast.86, s32[512]{0:T(512)S(1)} %get-tuple-element.13, s32[]{:T(128)} %constant.30.clone.1), kind=kCustom, calls=%fused_computation.51 | custom fusion | bytes 4100 | tf_op jit(solution)/shard_map/scatter | solution.py:50
  6.3 0.6 pad_add_fusion
  6.8 3.2 %all-to-all-start = ((s32[8,128,2]{1,0,2:T(8,128)}), s32[8,128,2]{1,0,2:T(8,128)S(1)}, u32[]{:S(2)}, u32[]{:S(2)}) async-start(s32[8,128,2]{1,0,2:T(8,128)} %pad_add_fusion), calls=%async_computation | async-start | bytes 16384 | tf_op jit(solution)/shard_map/all_to_all | solution.py:60
  10.1 0.7 fusion.22
  10.8 0.0 copy-done
  10.8 0.0 copy-start.2
  10.8 10.0 %fusion.5 = (f32[512]{0:T(512)S(1)}, f32[512]{0:T(512)S(1)}, f32[512,2048]{1,0:T(8,128)}) fusion(bf16[1,512,2048]{2,1,0:T(8,128)(2,1)} %param.7, f32[2048]{0:T(1024)} %bitcast.87, bf16[1,2048,2048]{2,1,0:T(8,128)(2,1)} %param.10, bf16[1,512,2048]{2,1,0:T(8,128)(2,1)S(1)} %copy-done), kind=kOutput, calls=%fused_computation.10 | convolution fusion | flops 4301257728 | bytes 16789504 | tf_op jit(solution)/shard_map/dot_general | solution.py:22
  20.8 5.8 %all-reduce = (f32[512]{0:T(512)S(1)}, f32[512]{0:T(512)S(1)}) all-reduce(f32[512]{0:T(512)S(1)} %get-tuple-element.6, f32[512]{0:T(512)S(1)} %get-tuple-element.5), channel_id=1, replica_groups=mesh['pipe'=2,'dp'=8,'mp'=2] {'mp'}, use_global_device_ids=true, to_apply=%region_7.8 | all-reduce | flops 1024 | bytes 8192 | tf_op jit(solution)/shard_map/psum | solution.py:27
  26.7 0.0 copy-done.2
  26.7 6.2 %convolution_convert_fusion = bf16[1024,2048]{1,0:T(8,128)(2,1)S(1)} fusion(f32[512,2048]{1,0:T(8,128)} %get-tuple-element.19, bf16[1,512,2048]{2,1,0:T(8,128)(2,1)} %param.11, bf16[1,512,2048]{2,1,0:T(8,128)(2,1)} %param.7, f32[512]{0:T(512)S(1)} %get-tuple-element.18, f32[2048]{0:T(1024)S(1)} %bitcast.88, f32[512]{0:T(512)S(1)} %get-tuple-element.17, ...), kind=kOutput, calls=%fused_computation.16 | convolution fusion | flops 2158493696 | bytes 12597248 | tf_op jit(solution)/shard_map/dot_general | solution.py:48
  32.9 0.4 slice_bitcast_fusion.1
  33.3 2.4 %pad_maximum_fusion = bf16[2,8,128,1024]{3,2,1,0:T(8,128)(2,1)} fusion(bf16[1,8,128,1024]{3,2,1,0:T(8,128)(2,1)S(1)} %get-tuple-element.12, bf16[1,8,128,1024]{3,2,1,0:T(8,128)(2,1)S(1)} %get-tuple-element.11), kind=kLoop, calls=%fused_computation.15 | loop fusion | flops 2097152 | bytes 8388608 | tf_op jit(solution)/shard_map/stack | solution.py:56
  35.7 0.0 all-to-all-done
  35.7 5.6 %all-to-all-start.2 = ((bf16[2,8,128,1024]{3,2,1,0:T(8,128)(2,1)}), bf16[2,8,128,1024]{3,2,1,0:T(8,128)(2,1)}, u32[]{:S(2)}, u32[]{:S(2)}) async-start(bf16[2,8,128,1024]{3,2,1,0:T(8,128)(2,1)} %pad_maximum_fusion), calls=%async_computation.2 | async-start | bytes 8388608 | tf_op jit(solution)/shard_map/all_to_all | solution.py:55
  41.3 0.6 copy.10
  41.9 3.9 %all-to-all-done.2 = bf16[2,8,128,1024]{3,2,1,0:T(8,128)(2,1)} async-done(((bf16[2,8,128,1024]{3,2,1,0:T(8,128)(2,1)}), bf16[2,8,128,1024]{3,2,1,0:T(8,128)(2,1)}, u32[]{:S(2)}, u32[]{:S(2)}) %all-to-all-start.2) | async-done | bytes 4194336 | tf_op jit(solution)/shard_map/all_to_all | solution.py:55
  45.8 6.4 %all-to-all-start.1 = ((s32[8,256,1]{1,2,0:T(1,128)}), s32[8,256,1]{1,2,0:T(1,128)S(1)}, u32[]{:S(2)}, u32[]{:S(2)}) async-start(s32[8,256,1]{1,2,0:T(1,128)} %copy.10), calls=%async_computation.1 | async-start | bytes 16384 | tf_op jit(solution)/shard_map/all_to_all | solution.py:64
  52.2 4.8 %copy.11 = bf16[2,8,128,1024]{3,2,0,1:T(8,128)(2,1)} copy(bf16[2,8,128,1024]{3,2,1,0:T(8,128)(2,1)} %all-to-all-done.2) | data formatting | bytes 8388608 | tf_op jit(solution)/shard_map/all_to_all | solution.py:55
  57.0 1.7 all-to-all-done.1
  58.7 97.4 %all_to_all.33 = bf16[8,256,1024]{2,1,0:T(8,128)(2,1)S(1)} all-to-all(bf16[8,256,1024]{2,1,0:T(8,128)(2,1)} %bitcast.74), channel_id=1, replica_groups=mesh['pipe'=2,'dp'=8,'mp'=2] {'dp'}, dimensions={0} | all-to-all | bytes 8388608 | tf_op jit(solution)/shard_map/all_to_all | solution.py:63
  156.1 17.4 %fusion.2 = f32[4016,1,1024]{2,0,1:T(8,128)S(1)} fusion(bf16[2048,1024]{1,0:T(8,128)(2,1)S(1)} %bitcast.76, s32[2048]{0:T(1024)S(1)} %bitcast.84), kind=kOutput, calls=%fused_computation.4 | convolution fusion | flops 16852549632 | bytes 20652032 | tf_op jit(solution)/shard_map/dot_general | solution.py:18
  173.5 0.0 copy-start.1
  173.5 63.9 %copy.12 = f32[4016,1,1024]{2,1,0:T(1,128)} copy(f32[4016,1,1024]{2,0,1:T(8,128)S(1)} %fusion.2) | data formatting | bytes 32899072 | tf_op jit(solution)/shard_map/reshape | solution.py:67
  237.4 0.0 copy-done.1
  (6 shorter events, 0.1 us)
Async XLA Ops:
  0.0 10.8 %copy-start = (bf16[1,512,2048]{2,1,0:T(8,128)(2,1)S(1)}, bf16[1,512,2048]{2,1,0:T(8,128)(2,1)}, u32[]{:S(2)}) copy-start(bf16[1,512,2048]{2,1,0:T(8,128)(2,1)} %param.9) | copy-start | bytes 6291460
  6.8 28.8 %all-to-all-start = ((s32[8,128,2]{1,0,2:T(8,128)}), s32[8,128,2]{1,0,2:T(8,128)S(1)}, u32[]{:S(2)}, u32[]{:S(2)}) async-start(s32[8,128,2]{1,0,2:T(8,128)} %pad_add_fusion), calls=%async_computation | async-start | bytes 16384 | tf_op jit(solution)/shard_map/all_to_all | solution.py:60
  10.8 15.9 %copy-start.2 = (f32[1,2048]{1,0:T(1,128)S(1)}, f32[1,2048]{1,0:T(1,128)}, u32[]{:S(2)}) copy-start(f32[1,2048]{1,0:T(1,128)} %param.8) | copy-start | bytes 24580
  35.7 10.1 %all-to-all-start.2 = ((bf16[2,8,128,1024]{3,2,1,0:T(8,128)(2,1)}), bf16[2,8,128,1024]{3,2,1,0:T(8,128)(2,1)}, u32[]{:S(2)}, u32[]{:S(2)}) async-start(bf16[2,8,128,1024]{3,2,1,0:T(8,128)(2,1)} %pad_maximum_fusion), calls=%async_computation.2 | async-start | bytes 8388608 | tf_op jit(solution)/shard_map/all_to_all | solution.py:55
  45.8 12.9 %all-to-all-start.1 = ((s32[8,256,1]{1,2,0:T(1,128)}), s32[8,256,1]{1,2,0:T(1,128)S(1)}, u32[]{:S(2)}, u32[]{:S(2)}) async-start(s32[8,256,1]{1,2,0:T(1,128)} %copy.10), calls=%async_computation.1 | async-start | bytes 16384 | tf_op jit(solution)/shard_map/all_to_all | solution.py:64
  173.5 63.9 %copy-start.1 = (bf16[1,512,2048]{2,1,0:T(8,128)(2,1)S(1)}, bf16[1,512,2048]{2,1,0:T(8,128)(2,1)}, u32[]{:S(2)}) copy-start(bf16[1,512,2048]{2,1,0:T(8,128)(2,1)} %param.9) | copy-start | bytes 6291460
